TPU v7x, 128 devices: a whole 4x4x4 slice. The times are simulated.
128 devices in a mesh: hi: 4 (over y), lo: 32 (over x, z, core).
Axes of the slice: x: 4, y: 4, z: 4, core: 2. Of those that a mesh axis runs over, the one named last changes fastest.
Arguments:
- initial_state: float32 [2, 16777216], P(None, ('hi', 'lo')), may hold values from -60 to 60
- gate_angles: float32 [2, 3, 24], replicated, may hold values from -3.140625 to 3.140625
- damp_qubits: int32 [2, 4], replicated, may hold values from 0 to 16, as said below
- kraus_branch: int32 [2, 4], replicated, may hold values 0 or 1
- damping: float32 [2, 4], replicated, may hold values from 0.1 to 0.6
Outputs:
- final_state: float32 [2, 16777216], P(None, ('hi', 'lo'))
- branch_weights: float32 [2, 4], replicated
Inputs may be any that keep to these rules, and one draw needn't show every extreme that they name: `damp_qubits`: the 8 entries are distinct qubits.
All inputs are finite; a program needn't handle non-finite values.
Results may differ from a plain program's by a relative error of at most 0.00022.
Values sent between devices are 32-bit elements; how exact they have to be, the bound alone decides.
No kernel may reach another device: no remote copies, remote signals or barrier semaphores. Data moves between devices by JAX's collectives and lax.ppermute only.
A program may use at most 128 MiB of HBM per device.

v0:
```python
import functools

import jax
import jax.numpy as jnp
from jax import lax
from jax.sharding import Mesh
from jax.sharding import PartitionSpec as P

HI_LO = ("hi", "lo_0", "lo_1", "lo_2")


epsilon = 1e-06


def one_axis_at_a_time(value, axes):
    return functools.reduce(lax.psum, axes, value)


def gate_table(angles):
    half_theta = angles[1] * 0.5
    cosine = jnp.cos(half_theta)
    sine = jnp.sin(half_theta)
    summed = (angles[0] + angles[2]) * 0.5
    differ = (angles[0] - angles[2]) * 0.5
    real_part = jnp.stack(
        [
            jnp.stack([jnp.cos(summed) * cosine, -jnp.cos(differ) * sine]),
            jnp.stack([jnp.cos(differ) * sine, jnp.cos(summed) * cosine]),
        ]
    )
    imag_part = jnp.stack(
        [
            jnp.stack([-jnp.sin(summed) * cosine, jnp.sin(differ) * sine]),
            jnp.stack([jnp.sin(differ) * sine, jnp.sin(summed) * cosine]),
        ]
    )
    return (real_part, imag_part)


def complex_times(coef_re, coef_im, values):
    return jnp.stack(
        [coef_re * values[0] - coef_im * values[1], coef_re * values[1] + coef_im * values[0]]
    )


def apply_gate(amplitudes, position, real_part, imag_part):
    total = amplitudes.shape[1]
    viewed = amplitudes.reshape(2, total >> position + 1, 2, 1 << position)
    zero_half = viewed[:, :, 0]
    one_half = viewed[:, :, 1]
    new_zero = complex_times(real_part[0, 0], imag_part[0, 0], zero_half) + complex_times(
        real_part[0, 1], imag_part[0, 1], one_half
    )
    new_one = complex_times(real_part[1, 0], imag_part[1, 0], zero_half) + complex_times(
        real_part[1, 1], imag_part[1, 1], one_half
    )
    return jnp.stack([new_zero, new_one], axis=2).reshape(2, total)


def low_block(amplitudes, real_part, imag_part):
    row_ids = lax.iota(jnp.int32, 128)[:, None]
    col_ids = lax.iota(jnp.int32, 128)[None, :]
    block_re = jnp.ones((128, 128), jnp.float32)
    block_im = jnp.zeros((128, 128), jnp.float32)
    for qubit_no in range(7):
        row_bit = jnp.bitwise_and(jnp.right_shift(row_ids, qubit_no), 1) == 0
        col_bit = jnp.bitwise_and(jnp.right_shift(col_ids, qubit_no), 1) == 0
        entry_re = jnp.where(
            row_bit,
            jnp.where(col_bit, real_part[0, 0, qubit_no], real_part[0, 1, qubit_no]),
            jnp.where(col_bit, real_part[1, 0, qubit_no], real_part[1, 1, qubit_no]),
        )
        entry_im = jnp.where(
            row_bit,
            jnp.where(col_bit, imag_part[0, 0, qubit_no], imag_part[0, 1, qubit_no]),
            jnp.where(col_bit, imag_part[1, 0, qubit_no], imag_part[1, 1, qubit_no]),
        )
        block_re, block_im = (
            block_re * entry_re - block_im * entry_im,
            block_re * entry_im + block_im * entry_re,
        )
    viewed = amplitudes.reshape(2, -1, 128)
    highest = lax.Precision.HIGHEST
    new_re = jnp.dot(viewed[0], block_re.T, precision=highest) - jnp.dot(
        viewed[1], block_im.T, precision=highest
    )
    new_im = jnp.dot(viewed[0], block_im.T, precision=highest) + jnp.dot(
        viewed[1], block_re.T, precision=highest
    )
    return jnp.stack([new_re, new_im]).reshape(2, -1)


def damp_step(amplitudes, target, rate, branch):
    total = amplitudes.shape[1]
    positions = lax.iota(jnp.int32, total)
    low_bit = jnp.bitwise_and(jnp.right_shift(positions, target), 1) == 0
    stride = jnp.left_shift(jnp.int32(1), target)
    shifted = jnp.roll(amplitudes, -stride, axis=1)
    lowered = jnp.where(low_bit, jnp.sqrt(rate) * shifted, jnp.zeros_like(amplitudes))
    kept = jnp.where(low_bit, amplitudes, jnp.sqrt(1.0 - rate) * amplitudes)
    return jnp.where(branch == 1, lowered, kept)


def regroup(amplitudes, devices):
    reshaped = amplitudes.reshape(2, devices, -1)
    moved = lax.all_to_all(reshaped, HI_LO, split_axis=1, concat_axis=1, tiled=True)
    return moved.reshape(2, -1)


def on_device(initial_state, gate_angles, damp_qubits, kraus_branch, damping):
    amplitudes = initial_state
    local_amps = amplitudes.shape[1]
    local_bits = local_amps.bit_length() - 1
    devices = lax.axis_size(HI_LO)
    global_bits = devices.bit_length() - 1
    whole = float(local_amps * devices)
    layer_count = gate_angles.shape[0]
    slot_count = damp_qubits.shape[1]
    weights = []
    for layer_no in range(layer_count):
        real_part, imag_part = gate_table(gate_angles[layer_no])
        amplitudes = low_block(amplitudes, real_part, imag_part)
        for qubit_no in range(7, local_bits):
            amplitudes = apply_gate(
                amplitudes, qubit_no, real_part[:, :, qubit_no], imag_part[:, :, qubit_no]
            )
        amplitudes = regroup(amplitudes, devices)
        for bit_no in range(global_bits):
            qubit_no = local_bits + bit_no
            amplitudes = apply_gate(
                amplitudes,
                local_bits - global_bits + bit_no,
                real_part[:, :, qubit_no],
                imag_part[:, :, qubit_no],
            )
        amplitudes = regroup(amplitudes, devices)
        partial_sums = [jnp.sum(amplitudes * amplitudes)]
        for slot_no in range(slot_count):
            amplitudes = damp_step(
                amplitudes,
                damp_qubits[layer_no, slot_no],
                damping[layer_no, slot_no],
                kraus_branch[layer_no, slot_no],
            )
            partial_sums.append(jnp.sum(amplitudes * amplitudes))
        totals = one_axis_at_a_time(jnp.stack(partial_sums), HI_LO) / whole
        factor = jnp.float32(1.0)
        for slot_no in range(slot_count):
            before = totals[slot_no] * factor * factor
            after = totals[slot_no + 1] * factor * factor
            weights.append(after / before)
            factor = factor * lax.rsqrt(after + epsilon)
        amplitudes = amplitudes * factor
    return (amplitudes, jnp.stack(weights).reshape(layer_count, slot_count))


def solution(mesh):
    split = Mesh(mesh.devices.reshape(mesh.shape["hi"], 4, 4, 2), ("hi", "lo_0", "lo_1", "lo_2"))
    return jax.shard_map(
        on_device,
        mesh=split,
        in_specs=(P(None, HI_LO), P(), P(), P(), P()),
        out_specs=(P(None, HI_LO), P()),
        check_vma=False,
    )
```

profile of v0, /device:TPU:1, one launch (start us, length us, event | category | flops | bytes accessed | tf_op | source)
XLA Modules:
  0.0 705.6 jit_solution(16786639409502999435)
XLA Ops:
  154.1 11.9 %all-to-all-start = ((f32[2,128,1024]{2,0,1:T(2,128)}), f32[2,128,1024]{2,0,1:T(2,128)S(1)}, u32[]{:S(2)}, u32[]{:S(2)}) async-start(f32[2,128,1024]{2,0,1:T(2,128)} %copy.92), calls=%async_computation | async-start | bytes 2097152 | tf_op jit(solution)/shard_map/all_to_all | solution.py:106
  309.3 5.5 multiply_subtract_fusion.74
  330.8 10.3 %all-to-all-start.1 = ((f32[2,128,1024]{2,0,1:T(2,128)}), f32[2,128,1024]{2,0,1:T(2,128)S(1)}, u32[]{:S(2)}, u32[]{:S(2)}) async-start(f32[2,128,1024]{2,0,1:T(2,128)} %copy.118), calls=%async_computation.1 | async-start | bytes 2097152 | tf_op jit(solution)/shard_map/all_to_all | solution.py:106
  341.8 18.3 %all-to-all-done.1 = f32[2,128,1024]{2,0,1:T(2,128)S(1)} async-done(((f32[2,128,1024]{2,0,1:T(2,128)}), f32[2,128,1024]{2,0,1:T(2,128)S(1)}, u32[]{:S(2)}, u32[]{:S(2)}) %all-to-all-start.1) | async-done | bytes 1048608 | tf_op jit(solution)/shard_map/all_to_all | solution.py:106
  360.1 6.2 multiply_reduce_fusion.8
  366.3 6.3 multiply_reduce_fusion.7
  372.6 6.3 multiply_reduce_fusion.6
  378.9 6.3 multiply_reduce_fusion.5
  390.0 7.0 psum.56
  397.0 6.7 psum.57
  403.7 6.4 psum.58
  410.1 9.4 %psum.59 = f32[5]{0:T(128)S(1)} all-reduce(f32[5]{0:T(128)S(1)} %psum.58), channel_id=1, replica_groups=mesh['hi'=4,'lo_0'=4,'lo_1'=4,'lo_2'=2] {'lo_2'}, use_global_device_ids=true, to_apply=%region_8.10 | all-reduce | flops 5 | bytes 40 | tf_op jit(solution)/shard_map/psum | solution.py:16
  510.1 5.5 multiply_subtract_fusion.30
  525.8 18.1 %all-to-all-done.2 = f32[2,128,1024]{2,0,1:T(2,128)S(1)} async-done(((f32[2,128,1024]{2,0,1:T(2,128)}), f32[2,128,1024]{2,0,1:T(2,128)S(1)}, u32[]{:S(2)}, u32[]{:S(2)}) %all-to-all-start.2) | async-done | bytes 1048608 | tf_op jit(solution)/shard_map/all_to_all | solution.py:106
  601.0 5.4 multiply_subtract_fusion.2
  619.6 16.3 %all-to-all-done.3 = f32[2,128,1024]{2,0,1:T(2,128)S(1)} async-done(((f32[2,128,1024]{2,0,1:T(2,128)}), f32[2,128,1024]{2,0,1:T(2,128)S(1)}, u32[]{:S(2)}, u32[]{:S(2)}) %all-to-all-start.3) | async-done | bytes 1048608 | tf_op jit(solution)/shard_map/all_to_all | solution.py:106
  635.9 6.2 multiply_reduce_fusion.3
  642.1 6.3 multiply_reduce_fusion.2
  648.4 6.3 multiply_reduce_fusion.1
  654.7 6.4 multiply_reduce_fusion
  666.1 7.0 psum.60
  673.1 6.7 psum.61
  679.8 6.4 psum.62
  687.6 9.2 %psum.63 = f32[5]{0:T(128)S(1)} all-reduce(f32[5]{0:T(128)S(1)} %psum.62), channel_id=1, replica_groups=mesh['hi'=4,'lo_0'=4,'lo_1'=4,'lo_2'=2] {'lo_2'}, use_global_device_ids=true, to_apply=%region_17.19 | all-reduce | flops 5 | bytes 40 | tf_op jit(solution)/shard_map/psum | solution.py:16
  (451 shorter events, 468.8 us)
Async XLA Ops:
  154.1 11.9 %copy-start = (s32[2,4]{1,0:T(2,128)S(1)}, s32[2,4]{1,0:T(2,128)}, u32[]{:S(2)}) copy-start(s32[2,4]{1,0:T(2,128)} %param.9) | copy-start | bytes 100
  154.1 15.5 %copy-start.1 = (f32[2,4]{1,0:T(2,128)S(1)}, f32[2,4]{1,0:T(2,128)}, u32[]{:S(2)}) copy-start(f32[2,4]{1,0:T(2,128)} %param.11) | copy-start | bytes 100
  154.1 44.7 %copy-start.2 = (s32[2,4]{1,0:T(2,128)S(1)}, s32[2,4]{1,0:T(2,128)}, u32[]{:S(2)}) copy-start(s32[2,4]{1,0:T(2,128)} %param.10) | copy-start | bytes 100
  154.1 108.9 %all-to-all-start = ((f32[2,128,1024]{2,0,1:T(2,128)}), f32[2,128,1024]{2,0,1:T(2,128)S(1)}, u32[]{:S(2)}, u32[]{:S(2)}) async-start(f32[2,128,1024]{2,0,1:T(2,128)} %copy.92), calls=%async_computation | async-start | bytes 2097152 | tf_op jit(solution)/shard_map/all_to_all | solution.py:106
  330.8 29.2 %all-to-all-start.1 = ((f32[2,128,1024]{2,0,1:T(2,128)}), f32[2,128,1024]{2,0,1:T(2,128)S(1)}, u32[]{:S(2)}, u32[]{:S(2)}) async-start(f32[2,128,1024]{2,0,1:T(2,128)} %copy.118), calls=%async_computation.1 | async-start | bytes 2097152 | tf_op jit(solution)/shard_map/all_to_all | solution.py:106
  520.9 22.9 %all-to-all-start.2 = ((f32[2,128,1024]{2,0,1:T(2,128)}), f32[2,128,1024]{2,0,1:T(2,128)S(1)}, u32[]{:S(2)}, u32[]{:S(2)}) async-start(f32[2,128,1024]{2,0,1:T(2,128)} %copy.159), calls=%async_computation.2 | async-start | bytes 2097152 | tf_op jit(solution)/shard_map/all_to_all | solution.py:106
  611.7 24.1 %all-to-all-start.3 = ((f32[2,128,1024]{2,0,1:T(2,128)}), f32[2,128,1024]{2,0,1:T(2,128)S(1)}, u32[]{:S(2)}, u32[]{:S(2)}) async-start(f32[2,128,1024]{2,0,1:T(2,128)} %copy.185), calls=%async_computation.3 | async-start | bytes 2097152 | tf_op jit(solution)/shard_map/all_to_all | solution.py:106
where the time goes:
time: 719 us; the launch traced here: 706 us
  other arithmetic  361 us (50%)
  local copies, waits for them, and re-layouts  159 us (22%)
  blocking collectives  58.9 us (8%)
  waiting for transfers between devices  52.6 us (7%)
  between operations  36.5 us (5%)
  starting transfers between devices  31.4 us (4%)
    sub x68, other arithmetic, complex_times(): coef_re * values[0] - coef_im * values[1]  198 us
    psum x8, blocking collectives, one_axis_at_a_time(): return functools.reduce(lax.psum, axes, value)  58.9 us
    all_to_all x4, waiting for transfers between devices, regroup(): lax.all_to_all(reshaped, HI_LO, split_axis=1, concat_axis=1, tiled=True)  52.6 us
    reduce_sum x8, other arithmetic, on_device(): partial_sums.append(jnp.sum(amplitudes * amplitudes))  50.3 us
    another operation x30, local copies, waits for them, and re-layouts, apply_gate(): viewed = amplitudes.reshape(2, total >> position + 1, 2, 1 << position)  38.1 us
    all_to_all x4, starting transfers between devices, regroup(): lax.all_to_all(reshaped, HI_LO, split_axis=1, concat_axis=1, tiled=True)  31.4 us
    slice x26, local copies, waits for them, and re-layouts, complex_times(): values[0]  24 us
    slice x34, local copies, waits for them, and re-layouts, apply_gate(): imag_part[0, 1]  22.2 us
  transfers between devices with their start and end apart: 4, of which 3 were waited for; matrix products, arithmetic and copies ran while one was open for 11% of the time, Pallas kernels for 0%

commit v1 on v0

v1 whole, which is shorter than its diff:
```python
import functools

import jax
import jax.numpy as jnp
from jax import lax
from jax.experimental import pallas as pl
from jax.experimental.pallas import tpu as pltpu
from jax.sharding import PartitionSpec as P

AXES = ("hi", "lo")
EPS = 1e-6
LANES = 128
ROWS = 16
MID = 8
f32 = jnp.float32
bf16 = jnp.bfloat16


def split(x):
    hi = x.astype(bf16)
    return hi, (x - hi.astype(f32)).astype(bf16)


def dot3(a, b):
    (ah, al), (bh, bl) = a, b
    d = functools.partial(jnp.dot, preferred_element_type=f32)
    return d(ah, bh) + (d(ah, bl) + d(al, bh))


def cmul(a, b):
    return a[0] * b[0] - a[1] * b[1], a[0] * b[1] + a[1] * b[0]


def matmul2(a, b):
    out = {}
    for i in range(2):
        for j in range(2):
            p, q = cmul(a[i, 0], b[0, j]), cmul(a[i, 1], b[1, j])
            out[i, j] = (p[0] + q[0], p[1] + q[1])
    return out


def scale2(k, u):
    k00, k01, k11 = k
    out = {}
    for j in range(2):
        out[0, j] = tuple(k00 * u[0, j][c] + k01 * u[1, j][c] for c in range(2))
        out[1, j] = tuple(k11 * u[1, j][c] for c in range(2))
    return out


def gates(angles_ref, layer):
    a, b, c = (angles_ref[layer, k : k + 1, :] for k in range(3))
    co, si = jnp.cos(b * 0.5), jnp.sin(b * 0.5)
    s, d = (a + c) * 0.5, (a - c) * 0.5
    cs, ss, cd, sd = jnp.cos(s), jnp.sin(s), jnp.cos(d), jnp.sin(d)
    return {
        (0, 0): (cs * co, -ss * co),
        (0, 1): (-cd * si, sd * si),
        (1, 0): (cd * si, sd * si),
        (1, 1): (cs * co, ss * co),
    }


def tables(angles_ref, targets, branches, rates):
    qubits = angles_ref.shape[2]
    lane = lax.broadcasted_iota(jnp.int32, (1, qubits), 1)
    one, zero = jnp.ones((1, qubits), f32), jnp.zeros((1, qubits), f32)
    u = [gates(angles_ref, layer) for layer in range(2)]
    krauses, first = [], zero > 1.0
    for layer in range(2):
        k00, k01, k11 = one, zero, one
        for slot in range(4):
            here = lane == targets[layer, slot]
            jump = branches[layer, slot] == 1
            g = jnp.full((1, qubits), rates[layer, slot], f32)
            k00 = jnp.where(here, jnp.where(jump, 0.0, 1.0), k00)
            k01 = jnp.where(here, jnp.where(jump, jnp.sqrt(g), 0.0), k01)
            k11 = jnp.where(here, jnp.where(jump, 0.0, jnp.sqrt(1.0 - g)), k11)
            if layer == 0:
                first = jnp.logical_or(first, here)
        krauses.append((k00, k01, k11))
    both = matmul2(u[1], u[0])
    v = {
        ij: tuple(jnp.where(first, u[0][ij][c], both[ij][c]) for c in range(2))
        for ij in both
    }
    m = scale2(krauses[1], matmul2(u[1], scale2(krauses[0], u[0])))
    return v, m


def entry(table, ij, c, qubit):
    return table[ij][c][:, qubit : qubit + 1]


def kron(table, start, transposed):
    rows = lax.broadcasted_iota(jnp.int32, (LANES, LANES), 0)
    cols = lax.broadcasted_iota(jnp.int32, (LANES, LANES), 1)
    if transposed:
        rows, cols = cols, rows
    acc = None
    for j in range(7):
        rb = jnp.bitwise_and(rows, 1 << j) == 0
        cb = jnp.bitwise_and(cols, 1 << j) == 0
        e = []
        for c in range(2):
            w = {
                ij: jnp.broadcast_to(entry(table, ij, c, start + j), (LANES, LANES))
                for ij in table
            }
            e.append(
                jnp.where(
                    rb,
                    jnp.where(cb, w[0, 0], w[0, 1]),
                    jnp.where(cb, w[1, 0], w[1, 1]),
                )
            )
        acc = tuple(e) if acc is None else cmul(acc, e)
    return acc


def left_big(w):
    re, im = w
    return jnp.concatenate(
        [jnp.concatenate([re, -im], 1), jnp.concatenate([im, re], 1)], 0
    )


def right_big(w):
    re, im = w
    return jnp.concatenate(
        [jnp.concatenate([re, im], 1), jnp.concatenate([-im, re], 1)], 0
    )


def mid_mix(load, store, coef):
    x = [load(q) for q in range(MID)]
    for j in range(3):
        for q in range(MID):
            if q >> j & 1:
                continue
            p = q | 1 << j
            x0, x1 = x[q], x[p]
            new = []
            for i in range(2):
                a, b = cmul(coef(j, i, 0), x0), cmul(coef(j, i, 1), x1)
                new.append((a[0] + b[0], a[1] + b[1]))
            x[q], x[p] = new
    for q in range(MID):
        store(q, x[q])


def strided(start, stride):
    return pl.ds(start, LANES, stride=stride)


def right_stage(x_ref, stride, weights, tmp_ref):
    for q in range(MID):
        x = jnp.concatenate(
            [x_ref[strided(2 * q + c, stride), :] for c in range(2)], 1
        )
        tmp_ref[q] = dot3(split(x), weights)


def mid_stage(tmp_ref, coef):
    def body(i, _):
        at = pl.ds(pl.multiple_of(i * 8, 8), 8)

        def load(q):
            return tmp_ref[q, at, :LANES], tmp_ref[q, at, LANES:]

        def store(q, value):
            tmp_ref[q, at, :LANES], tmp_ref[q, at, LANES:] = value

        mid_mix(load, store, coef)
        return 0

    lax.fori_loop(0, LANES // 8, body, 0, unroll=True)


def left_pair(weights, a, b):
    x = jnp.concatenate(
        [jnp.concatenate([a[c], b[c]], 1) for c in range(2)], 0
    )
    y = dot3(weights, split(x))
    return [
        tuple(y[c * LANES : (c + 1) * LANES, p * LANES : (p + 1) * LANES] for c in range(2))
        for p in range(2)
    ]


def level_sums(squares, targets, branches, rates, layer):
    lane = lax.broadcasted_iota(jnp.int32, (LANES, LANES), 1)
    row = lax.broadcasted_iota(jnp.int32, (LANES, LANES), 0)
    weight = jnp.ones((LANES, LANES), f32)
    wq = [jnp.float32(1.0)] * MID
    out = []

    def total(v):
        return jnp.sum(jnp.sum(v, axis=0, keepdims=True), axis=1, keepdims=True)

    for slot in range(5):
        mixed = wq[0] * squares[0]
        for q in range(1, MID):
            mixed = mixed + wq[q] * squares[q]
        out.append(total(mixed * weight))
        if slot == 4:
            break
        t = targets[layer, slot]
        g = rates[layer, slot]
        jump = branches[layer, slot] == 1
        f0 = jnp.where(jump, 0.0, 1.0)
        f1 = jnp.where(jump, g, 1.0 - g)
        low, mid = t < 7, jnp.logical_and(t >= 7, t < 10)
        index = jnp.where(low, lane, row)
        shift = jnp.where(low, t, jnp.maximum(t - 10, 0))
        bit = jnp.bitwise_and(jnp.right_shift(index, shift), 1)
        factor = jnp.where(bit == 1, f1, f0)
        weight = weight * jnp.where(mid, jnp.ones_like(factor), factor)
        tm = jnp.where(mid, t - 7, 0)
        wq = [
            w * jnp.where(mid, jnp.where(jnp.bitwise_and(jnp.right_shift(q, tm), 1) == 1, f1, f0), 1.0)
            for q, w in enumerate(wq)
        ]
    return out, weight, wq


def prep_kernel(x_ref, angles_ref, targets, branches, rates,
                g_ref, low_ref, top_ref, mid_ref, sums_ref, tmp_ref):
    v, m = tables(angles_ref, targets, branches, rates)
    g_ref[0], g_ref[1] = split(left_big(kron(m, 17, False)))
    low_ref[0], low_ref[1] = split(right_big(kron(m, 0, True)))
    top_ref[0], top_ref[1] = split(left_big(kron(m, 10, False)))
    for j in range(3):
        for i in range(2):
            for k in range(2):
                for c in range(2):
                    r = ((j * 2 + i) * 2 + k) * 2 + c
                    mid_ref[r : r + 1, :] = jnp.broadcast_to(
                        entry(m, (i, k), c, 7 + j), (1, LANES)
                    )
    v_low = split(right_big(kron(v, 0, True)))
    v_top = split(left_big(kron(v, 10, False)))
    right_stage(x_ref, ROWS, v_low, tmp_ref)
    v_mid = {
        (j, i, k, c): jnp.broadcast_to(entry(v, (i, k), c, 7 + j), (8, LANES))
        for j in range(3) for i in range(2) for k in range(2) for c in range(2)
    }
    mid_stage(tmp_ref, lambda j, i, k: (v_mid[j, i, k, 0], v_mid[j, i, k, 1]))
    psi = []
    for q in range(0, MID, 2):
        ab = [(tmp_ref[p, :, :LANES], tmp_ref[p, :, LANES:]) for p in (q, q + 1)]
        for p, y in zip((q, q + 1), left_pair(v_top, *ab)):
            tmp_ref[p, :, :LANES], tmp_ref[p, :, LANES:] = y
    squares = [
        tmp_ref[q, :, :LANES] * tmp_ref[q, :, :LANES]
        + tmp_ref[q, :, LANES:] * tmp_ref[q, :, LANES:]
        for q in range(MID)
    ]
    first, weight, wq = level_sums(squares, targets, branches, rates, 0)
    kept = first[4]
    alpha = jnp.where(kept > 0.0, lax.rsqrt(jnp.maximum(kept, 1e-37)), 0.0)
    root = jnp.sqrt(weight)
    later = []
    for q in range(MID):
        r = root * jnp.sqrt(jnp.full((1, LANES), wq[q], f32)) * alpha
        re, im = tmp_ref[q, :, :LANES] * r, tmp_ref[q, :, LANES:] * r
        later.append(re * re + im * im)
    second, _, _ = level_sums(later, targets, branches, rates, 1)
    base = jnp.where(second[0] > 0.0, second[0], 1.0)
    values = first + [s / base for s in second[1:]]
    lane = lax.broadcasted_iota(jnp.int32, (8, LANES), 1)
    packed = jnp.zeros((8, LANES), f32)
    for k, s in enumerate(values):
        packed = jnp.where(lane == k, s, packed)
    sums_ref[...] = packed


def global_kernel(x_ref, g_ref, sums_ref, out_ref, *, stride):
    weights = (g_ref[0], g_ref[1])
    for q in range(0, MID, 2):
        ab = [
            tuple(x_ref[strided(2 * p + c, ROWS), :] for c in range(2))
            for p in (q, q + 1)
        ]
        for p, y in zip((q, q + 1), left_pair(weights, *ab)):
            for c in range(2):
                out_ref[strided(2 * p + c, stride), :] = y[c]
    out_ref[strided(ROWS, stride), :] = jnp.broadcast_to(
        sums_ref[0:1, :], (LANES, LANES)
    )


def final_kernel(x_ref, low_ref, top_ref, mid_ref, out_ref, weights_ref, tmp_ref, *, stride, whole):
    parts = x_ref[strided(ROWS, stride), :]
    totals = jnp.sum(parts, axis=0, keepdims=True)
    kept = parts[:, 4:5]
    kept_total = jnp.maximum(totals[:, 4:5], 1e-37)
    ratios = jnp.sum(parts * (kept / kept_total), axis=0, keepdims=True)
    lane = lax.broadcasted_iota(jnp.int32, (1, LANES), 1)
    row = jnp.zeros((1, LANES), f32)
    factors = []
    mean = [totals[:, k : k + 1] / whole for k in range(5)]
    for layer in range(2):
        factor = jnp.ones((1, 1), f32)
        for slot in range(4):
            before = mean[slot] * factor * factor
            after = mean[slot + 1] * factor * factor
            row = jnp.where(lane == layer * 4 + slot, after / before, row)
            factor = factor * lax.rsqrt(after + EPS)
        factors.append(factor)
        if layer == 0:
            start = mean[4] * factor * factor
            mean = [start] + [start * ratios[:, 5 + k : 6 + k] for k in range(4)]
    weights_ref[...] = jnp.broadcast_to(row, (8, LANES))
    right_stage(x_ref, stride, (low_ref[0], low_ref[1]), tmp_ref)

    def coef(j, i, k):
        r = ((j * 2 + i) * 2 + k) * 2
        return mid_ref[r : r + 1, :], mid_ref[r + 1 : r + 2, :]

    mid_stage(tmp_ref, coef)
    top = (top_ref[0], top_ref[1])
    for q in range(0, MID, 2):
        ab = [(tmp_ref[p, :, :LANES], tmp_ref[p, :, LANES:]) for p in (q, q + 1)]
        for p, y in zip((q, q + 1), left_pair(top, *ab)):
            for c in range(2):
                out_ref[strided(2 * p + c, ROWS), :] = y[c] * factors[0] * factors[1]


def on_device(initial_state, gate_angles, damp_qubits, kraus_branch, damping):
    devices = lax.axis_size(AXES)
    local = initial_state.shape[1]
    whole = float(local * devices)
    stride = ROWS + 1
    vmem = pl.BlockSpec(memory_space=pltpu.VMEM)
    smem = pl.BlockSpec(memory_space=pltpu.SMEM)
    rows = local * 2 // LANES
    x = initial_state.reshape(2, rows // 2, LANES).transpose(1, 0, 2)
    x = x.reshape(devices, ROWS, LANES)
    swapped = lax.all_to_all(x, AXES, split_axis=0, concat_axis=0, tiled=True)
    big = jax.ShapeDtypeStruct((2, 256, 256), bf16)
    g, low, top, mid, sums = pl.pallas_call(
        prep_kernel,
        out_shape=(big, big, big,
                   jax.ShapeDtypeStruct((24, LANES), f32),
                   jax.ShapeDtypeStruct((8, LANES), f32)),
        in_specs=[vmem, vmem, smem, smem, smem],
        out_specs=(vmem,) * 5,
        scratch_shapes=[pltpu.VMEM((MID, LANES, 2 * LANES), f32)],
        cost_estimate=pl.CostEstimate(flops=2_000_000_000, bytes_accessed=2_000_000, transcendentals=0),
        name="prep",
    )(x.reshape(rows, LANES), gate_angles, damp_qubits, kraus_branch, damping)
    mixed = pl.pallas_call(
        functools.partial(global_kernel, stride=stride),
        out_shape=jax.ShapeDtypeStruct((devices * stride, LANES), f32),
        in_specs=[vmem] * 3,
        out_specs=vmem,
        cost_estimate=pl.CostEstimate(flops=400_000_000, bytes_accessed=2_000_000, transcendentals=0),
        name="global_gates",
    )(swapped.reshape(rows, LANES), g, sums)
    back = lax.all_to_all(
        mixed.reshape(devices, 1, stride * LANES), AXES, split_axis=0, concat_axis=0, tiled=True
    )
    out, weights = pl.pallas_call(
        functools.partial(final_kernel, stride=stride, whole=whole),
        out_shape=(jax.ShapeDtypeStruct((rows, LANES), f32),
                   jax.ShapeDtypeStruct((8, LANES), f32)),
        in_specs=[vmem] * 4,
        out_specs=(vmem, vmem),
        scratch_shapes=[pltpu.VMEM((MID, LANES, 2 * LANES), f32)],
        cost_estimate=pl.CostEstimate(flops=800_000_000, bytes_accessed=2_000_000, transcendentals=0),
        name="local_gates",
    )(back.reshape(devices * stride, LANES), low, top, mid)
    out = out.reshape(rows // 2, 2, LANES).transpose(1, 0, 2).reshape(2, local)
    return out, weights[0, : damp_qubits.size].reshape(damp_qubits.shape)


def solution(mesh):
    return jax.shard_map(
        on_device,
        mesh=mesh,
        in_specs=(P(None, AXES), P(), P(), P(), P()),
        out_specs=(P(None, AXES), P()),
        check_vma=False,
    )
```

time: 719 us -> 66.7 us (0.09); the launches traced: 706 us -> 66.3 us
  other arithmetic: 361 us -> 0 us
  local copies, waits for them, and re-layouts: 159 us -> 2.91 us
  waiting for transfers between devices: 52.6 us -> 12.9 us
  between operations: 36.5 us -> 0.66 us
  blocking collectives: 58.9 us -> 25.5 us
  starting transfers between devices: 31.4 us -> 11.5 us
  Pallas kernels: 0 us -> 12.8 us
    sub x68 -> x0, other arithmetic: 198 us -> none  [complex_times(): coef_re * values[0] - coef_im * values[1]]
    slice x111 -> x1, local copies, waits for them, and re-layouts: 81.3 us -> 0.69 us  [on_device(): return (out, weights[0, :damp_qubits.size].reshape(damp_qubits.shape))]
    another operation x67 -> x1, local copies, waits for them, and re-layouts: 77 us -> 0.64 us  [on_device(): return (out, weights[0, :damp_qubits.size].reshape(damp_qubits.shape))]
    select_n x56 -> x0, other arithmetic: 70 us -> none  [the longest x14 17.7 us: low_block(): jnp.where(col_bit, imag_part[1, 0, qubit_no], imag_part[1, 1, qubit_no])]
    psum x8 -> x0, blocking collectives: 58.9 us -> none  [one_axis_at_a_time(): return functools.reduce(lax.psum, axes, value)]
    reduce_sum x10 -> x0, other arithmetic: 53.8 us -> none  [the longest x8 50.3 us: on_device(): partial_sums.append(jnp.sum(amplitudes * amplitudes))]
    all_to_all x4 -> x1, waiting for transfers between devices: 52.6 us -> 12.9 us  [on_device(): swapped = lax.all_to_all(x, AXES, split_axis=0, concat_axis=0, tiled=True)]
    all_to_all x0 -> x1, blocking collectives: none -> 25.5 us  [on_device(): lax.all_to_all(mixed.reshape(devices, 1, stride * LANES), AXES, split_axi...]
  transfers between devices with their start and end apart: 4 -> 1, of which waited for: 3 -> 1; matrix products, arithmetic and copies ran while one was open for 11% -> 1% of each run, Pallas kernels for 0% -> 8%
where the time goes in v1:
time: 66.7 us; the launch traced here: 66.3 us
  blocking collectives  25.5 us (38%)
  waiting for transfers between devices  12.9 us (19%)
  Pallas kernels  12.8 us (19%)
  starting transfers between devices  11.5 us (17%)
  local copies, waits for them, and re-layouts  2.91 us (4%)
    all_to_all x1, blocking collectives, on_device(): lax.all_to_all(mixed.reshape(devices, 1, stride * LANES), AXES, split_axi...  25.5 us
    all_to_all x1, waiting for transfers between devices, on_device(): swapped = lax.all_to_all(x, AXES, split_axis=0, concat_axis=0, tiled=True)  12.9 us
    all_to_all x1, starting transfers between devices, on_device(): swapped = lax.all_to_all(x, AXES, split_axis=0, concat_axis=0, tiled=True)  11.5 us
    pallas_call x1, Pallas kernels, on_device(): pl.pallas_call(prep_kernel, out_shape=(big, big, big, jax.ShapeDtypeStruc...  5.49 us
    pallas_call x1, Pallas kernels, on_device(): pl.pallas_call(functools.partial(final_kernel, stride=stride, whole=whole...  4.18 us
    pallas_call x1, Pallas kernels, on_device(): pl.pallas_call(functools.partial(global_kernel, stride=stride), out_shape...  3.16 us
    unnamed x5, local copies, waits for them, and re-layouts  1.57 us
  transfers between devices with their start and end apart: 1, of which 1 were waited for; matrix products, arithmetic and copies ran while one was open for 1% of the time, Pallas kernels for 8%

profile of v1, /device:TPU:1, one launch (start us, length us, event | category | flops | bytes accessed | tf_op | source)
XLA Modules:
  0.0 66.3 jit_solution(5296499285800934210)
XLA Ops:
  0.6 0.0 copy-start.1
  0.6 11.5 %all-to-all-start = ((f32[128,16,128]{2,1,0:T(8,128)}), f32[128,16,128]{2,1,0:T(8,128)S(1)}, u32[]{:S(2)}, u32[]{:S(2)}) async-start(f32[128,16,128]{2,1,0:T(8,128)} %bitcast.18), calls=%async_computation | async-start | bytes 2097152 | tf_op jit(solution)/shard_map/all_to_all | solution.py:341
  12.1 0.0 copy-done.1
  12.1 0.6 copy.11.angles_ref
  12.7 5.5 %prep.1 = (bf16[2,256,256]{2,1,0:T(8,128)(2,1)}, bf16[2,256,256]{2,1,0:T(8,128)(2,1)}, bf16[2,256,256]{2,1,0:T(8,128)(2,1)}, f32[24,128]{1,0:T(8,128)}, f32[8,128]{1,0:T(8,128)}) custom-call(f32[2048,128]{1,0:T(8,128)} %bitcast.19, f32[2,3,24]{2,1,0:T(4,128)} %copy.11.angles_ref, s32[2,4]{1,0:T(2,128)} %targets.1, s32[2,4]{1,0:T(2,128)} %branches.1, ...), custom_call_target="tpu_custom_call" | custom-call | flops 2000000000 | bytes 2000000 | tf_op jit(solution)/shard_map/prep/pallas_call | solution.py:343
  18.2 12.9 %all-to-all-done = f32[128,16,128]{2,1,0:T(8,128)S(1)} async-done(((f32[128,16,128]{2,1,0:T(8,128)}), f32[128,16,128]{2,1,0:T(8,128)S(1)}, u32[]{:S(2)}, u32[]{:S(2)}) %all-to-all-start) | async-done | bytes 1048608 | tf_op jit(solution)/shard_map/all_to_all | solution.py:341
  31.2 0.0 copy-start
  31.2 1.0 %copy-done = f32[128,16,128]{2,1,0:T(8,128)} copy-done((f32[128,16,128]{2,1,0:T(8,128)}, f32[128,16,128]{2,1,0:T(8,128)S(1)}, u32[]{:S(2)}) %copy-start) | copy-done | bytes 1048600
  32.1 3.2 %global_gates.1 = f32[2176,128]{1,0:T(8,128)} custom-call(f32[2048,128]{1,0:T(8,128)} %bitcast.16, bf16[2,256,256]{2,1,0:T(8,128)(2,1)} %get-tuple-element.9.g_ref, f32[8,128]{1,0:T(8,128)} %get-tuple-element.10.sums_ref), custom_call_target="tpu_custom_call" | custom-call | flops 400000000 | bytes 2000000 | tf_op jit(solution)/shard_map/global_gates/pallas_call | solution.py:354
  35.3 25.5 %all_to_all.10 = f32[128,1,2176]{2,1,0:T(1,128)} all-to-all(f32[128,1,2176]{2,1,0:T(1,128)} %bitcast.15), channel_id=1, replica_groups=mesh['hi'=4,'lo'=32] {'hi','lo'}, dimensions={0} | all-to-all | bytes 2228224 | tf_op jit(solution)/shard_map/all_to_all | solution.py:362
  60.8 4.2 %local_gates.1 = (f32[2048,128]{1,0:T(8,128)}, f32[8,128]{1,0:T(8,128)}) custom-call(f32[2176,128]{1,0:T(8,128)} %bitcast.17, bf16[2,256,256]{2,1,0:T(8,128)(2,1)} %get-tuple-element.11.low_ref, bf16[2,256,256]{2,1,0:T(8,128)(2,1)} %get-tuple-element.12.top_ref, f32[24,128]{1,0:T(8,128)} %get-tuple-element.13.mid_ref), custom_call_target="tpu_custom_call" | custom-call | flops 800000000 | bytes 2000000 | tf_op jit(solution)/shard_map/local_gates/pallas_call | solution.py:365
  65.0 0.7 %slice_reduce_fusion = f32[8]{0:T(128)S(1)} fusion(f32[8,128]{1,0:T(8,128)} %get-tuple-element.15), kind=kLoop, calls=%fused_computation | loop fusion | bytes 64 | tf_op jit(solution)/shard_map/slice | solution.py:376
  65.7 0.6 reshape_squeeze.3
Async XLA Ops:
  0.6 11.5 %copy-start.1 = (f32[2,3,24]{2,0,1:T(2,128)S(1)}, f32[2,3,24]{2,0,1:T(2,128)}, u32[]{:S(2)}) copy-start(f32[2,3,24]{2,0,1:T(2,128)} %param.6) | copy-start | bytes 1732
  0.6 30.5 %all-to-all-start = ((f32[128,16,128]{2,1,0:T(8,128)}), f32[128,16,128]{2,1,0:T(8,128)S(1)}, u32[]{:S(2)}, u32[]{:S(2)}) async-start(f32[128,16,128]{2,1,0:T(8,128)} %bitcast.18), calls=%async_computation | async-start | bytes 2097152 | tf_op jit(solution)/shard_map/all_to_all | solution.py:341
  31.2 1.0 %copy-start = (f32[128,16,128]{2,1,0:T(8,128)}, f32[128,16,128]{2,1,0:T(8,128)S(1)}, u32[]{:S(2)}) copy-start(f32[128,16,128]{2,1,0:T(8,128)S(1)} %all-to-all-done) | copy-start | bytes 3145732

commit v2 on v1

--- a/solution.py
+++ b/solution.py
@@ -312,7 +312,8 @@
         if layer == 0:
             start = mean[4] * factor * factor
             mean = [start] + [start * ratios[:, 5 + k : 6 + k] for k in range(4)]
-    weights_ref[...] = jnp.broadcast_to(row, (8, LANES))
+    weights_ref[0:1, :] = row[:, 0:4]
+    weights_ref[1:2, :] = row[:, 4:8]
     right_stage(x_ref, stride, (low_ref[0], low_ref[1]), tmp_ref)
 
     def coef(j, i, k):
@@ -339,41 +340,46 @@
     x = initial_state.reshape(2, rows // 2, LANES).transpose(1, 0, 2)
     x = x.reshape(devices, ROWS, LANES)
     swapped = lax.all_to_all(x, AXES, split_axis=0, concat_axis=0, tiled=True)
-    big = jax.ShapeDtypeStruct((2, 256, 256), bf16)
+    big = pltpu.VMEM((2, 256, 256), bf16)
+    near = functools.partial(pltpu.with_memory_space_constraint, memory_space=pltpu.VMEM)
+    params = pltpu.CompilerParams(vmem_limit_bytes=24 << 20)
     g, low, top, mid, sums = pl.pallas_call(
         prep_kernel,
         out_shape=(big, big, big,
-                   jax.ShapeDtypeStruct((24, LANES), f32),
-                   jax.ShapeDtypeStruct((8, LANES), f32)),
+                   pltpu.VMEM((24, LANES), f32),
+                   pltpu.VMEM((8, LANES), f32)),
         in_specs=[vmem, vmem, smem, smem, smem],
         out_specs=(vmem,) * 5,
         scratch_shapes=[pltpu.VMEM((MID, LANES, 2 * LANES), f32)],
         cost_estimate=pl.CostEstimate(flops=2_000_000_000, bytes_accessed=2_000_000, transcendentals=0),
+        compiler_params=params,
         name="prep",
     )(x.reshape(rows, LANES), gate_angles, damp_qubits, kraus_branch, damping)
     mixed = pl.pallas_call(
         functools.partial(global_kernel, stride=stride),
-        out_shape=jax.ShapeDtypeStruct((devices * stride, LANES), f32),
+        out_shape=pltpu.VMEM((devices * stride, LANES), f32),
         in_specs=[vmem] * 3,
         out_specs=vmem,
         cost_estimate=pl.CostEstimate(flops=400_000_000, bytes_accessed=2_000_000, transcendentals=0),
+        compiler_params=params,
         name="global_gates",
-    )(swapped.reshape(rows, LANES), g, sums)
+    )(near(swapped.reshape(rows, LANES)), near(g), near(sums))
     back = lax.all_to_all(
         mixed.reshape(devices, 1, stride * LANES), AXES, split_axis=0, concat_axis=0, tiled=True
     )
     out, weights = pl.pallas_call(
         functools.partial(final_kernel, stride=stride, whole=whole),
         out_shape=(jax.ShapeDtypeStruct((rows, LANES), f32),
-                   jax.ShapeDtypeStruct((8, LANES), f32)),
+                   jax.ShapeDtypeStruct(damp_qubits.shape, f32)),
         in_specs=[vmem] * 4,
         out_specs=(vmem, vmem),
         scratch_shapes=[pltpu.VMEM((MID, LANES, 2 * LANES), f32)],
         cost_estimate=pl.CostEstimate(flops=800_000_000, bytes_accessed=2_000_000, transcendentals=0),
+        compiler_params=params,
         name="local_gates",
-    )(back.reshape(devices * stride, LANES), low, top, mid)
+    )(near(back.reshape(devices * stride, LANES)), near(low), near(top), near(mid))
     out = out.reshape(rows // 2, 2, LANES).transpose(1, 0, 2).reshape(2, local)
-    return out, weights[0, : damp_qubits.size].reshape(damp_qubits.shape)
+    return out, weights
 
 
 def solution(mesh):

time: 66.7 us -> 59.1 us (0.89)
  Pallas kernels: 12.8 us -> 7.85 us
  local copies, waits for them, and re-layouts: 2.91 us -> 0.02 us
  waiting for transfers between devices: 12.9 us -> 14.7 us
  blocking collectives: 25.5 us -> 24.1 us
    pallas_call x1, Pallas kernels: 3.16 us -> 0.81 us  [on_device(): pl.pallas_call(functools.partial(global_kernel, stride=stride), out_shape...]
    all_to_all x1, waiting for transfers between devices: 12.9 us -> 14.7 us  [on_device(): swapped = lax.all_to_all(x, AXES, split_axis=0, concat_axis=0, tiled=True)]
    unnamed x5 -> x11, local copies, waits for them, and re-layouts: 1.57 us -> 0.02 us
    all_to_all x1, blocking collectives: 25.5 us -> 24.1 us  [on_device(): lax.all_to_all(mixed.reshape(devices, 1, stride * LANES), AXES, split_axi...]
    pallas_call x1, Pallas kernels: 4.18 us -> 2.82 us  [on_device(): pl.pallas_call(functools.partial(final_kernel, stride=stride, whole=whole...]
    pallas_call x1, Pallas kernels: 5.49 us -> 4.22 us  [on_device(): pl.pallas_call(prep_kernel, out_shape=(big, big, big, pltpu.VMEM((24, LAN...]
    slice x1 -> x0, local copies, waits for them, and re-layouts: 0.69 us -> none  [on_device(): return (out, weights[0, :damp_qubits.size].reshape(damp_qubits.shape))]
  transfers between devices with their start and end apart: 1 -> 1, of which waited for: 1 -> 1; matrix products, arithmetic and copies ran while one was open for 1% -> 0% of each run, Pallas kernels for 8% -> 7%
where the time goes in v2:
time: 59.1 us; the launch traced here: 58.9 us
  blocking collectives  24.1 us (41%)
  waiting for transfers between devices  14.7 us (25%)
  starting transfers between devices  11.5 us (19%)
  Pallas kernels  7.85 us (13%)
  between operations  0.74 us (1%)
    all_to_all x1, blocking collectives, on_device(): lax.all_to_all(mixed.reshape(devices, 1, stride * LANES), AXES, split_axi...  24.1 us
    all_to_all x1, waiting for transfers between devices, on_device(): swapped = lax.all_to_all(x, AXES, split_axis=0, concat_axis=0, tiled=True)  14.7 us
    all_to_all x1, starting transfers between devices, on_device(): swapped = lax.all_to_all(x, AXES, split_axis=0, concat_axis=0, tiled=True)  11.5 us
    pallas_call x1, Pallas kernels, on_device(): pl.pallas_call(prep_kernel, out_shape=(big, big, big, pltpu.VMEM((24, LAN...  4.22 us
    pallas_call x1, Pallas kernels, on_device(): pl.pallas_call(functools.partial(final_kernel, stride=stride, whole=whole...  2.82 us
  transfers between devices with their start and end apart: 1, of which 1 were waited for; matrix products, arithmetic and copies ran while one was open for 0% of the time, Pallas kernels for 7%

profile of v2, /device:TPU:1, one launch (start us, length us, event | category | flops | bytes accessed | tf_op | source)
XLA Modules:
  0.0 58.9 jit_solution(18304518660101080336)
XLA Ops:
  0.6 0.0 copy-start
  0.6 0.0 copy-start.4
  0.7 0.0 copy-start.3
  0.7 0.0 copy-start.2
  0.7 0.0 copy-start.1
  0.7 11.5 %all-to-all-start = ((f32[128,16,128]{2,1,0:T(8,128)}), f32[128,16,128]{2,1,0:T(8,128)S(1)}, u32[]{:S(2)}, u32[]{:S(2)}) async-start(f32[128,16,128]{2,1,0:T(8,128)} %bitcast.18), calls=%async_computation | async-start | bytes 2097152 | tf_op jit(solution)/shard_map/all_to_all | solution.py:342
  12.2 0.0 copy-done.4
  12.2 0.0 copy-done
  12.2 0.0 copy-done.3
  12.2 0.0 copy-done.2
  12.2 0.0 copy-done.1
  12.2 4.2 %prep.1 = (bf16[2,256,256]{2,1,0:T(8,128)(2,1)S(1)}, bf16[2,256,256]{2,1,0:T(8,128)(2,1)S(1)}, bf16[2,256,256]{2,1,0:T(8,128)(2,1)S(1)}, f32[24,128]{1,0:T(8,128)S(1)}, f32[8,128]{1,0:T(8,128)S(1)}) custom-call(f32[2048,128]{1,0:T(8,128)S(1)} %bitcast.19, f32[2,3,24]{2,1,0:T(4,128)S(1)} %copy.11.angles_ref, s32[2,4]{1,0:T(2,128)S(1)} %copy-done.1, ...), custom_call_target="tpu_custom_call" | custom-call | flops 2000000000 | bytes 2000000 | tf_op jit(solution)/shard_map/prep/pallas_call | solution.py:346
  16.5 14.7 %all-to-all-done = f32[128,16,128]{2,1,0:T(8,128)S(1)} async-done(((f32[128,16,128]{2,1,0:T(8,128)}), f32[128,16,128]{2,1,0:T(8,128)S(1)}, u32[]{:S(2)}, u32[]{:S(2)}) %all-to-all-start) | async-done | bytes 1048608 | tf_op jit(solution)/shard_map/all_to_all | solution.py:342
  31.2 0.8 %global_gates.1 = f32[2176,128]{1,0:T(8,128)S(1)} custom-call(f32[2048,128]{1,0:T(8,128)S(1)} %bitcast.16, bf16[2,256,256]{2,1,0:T(8,128)(2,1)S(1)} %get-tuple-element.9.g_ref, f32[8,128]{1,0:T(8,128)S(1)} %get-tuple-element.10.sums_ref), custom_call_target="tpu_custom_call" | custom-call | flops 400000000 | bytes 2000000 | tf_op jit(solution)/shard_map/global_gates/pallas_call | solution.py:358
  32.0 24.1 %all_to_all.10 = f32[128,1,2176]{2,1,0:T(1,128)S(1)} all-to-all(f32[128,1,2176]{2,1,0:T(1,128)S(1)} %bitcast.15), channel_id=1, replica_groups=mesh['hi'=4,'lo'=32] {'hi','lo'}, dimensions={0} | all-to-all | bytes 2228224 | tf_op jit(solution)/shard_map/all_to_all | solution.py:367
  56.1 2.8 %local_gates.1 = (f32[2048,128]{1,0:T(8,128)}, f32[2,4]{1,0:T(2,128)}) custom-call(f32[2176,128]{1,0:T(8,128)S(1)} %bitcast.17, bf16[2,256,256]{2,1,0:T(8,128)(2,1)S(1)} %get-tuple-element.11.low_ref, bf16[2,256,256]{2,1,0:T(8,128)(2,1)S(1)} %get-tuple-element.12.top_ref, f32[24,128]{1,0:T(8,128)S(1)} %get-tuple-element.13.mid_ref), custom_call_target="tpu_custom_call" | custom-call | flops 800000000 | bytes 2000000 | tf_op jit(solution)/shard_map/local_gates/pallas_call | solution.py:370
  (1 shorter events, 0.0 us)
Async XLA Ops:
  0.6 11.6 %copy-start = (f32[2,131072]{1,0:T(2,128)S(1)}, f32[2,131072]{1,0:T(2,128)}, u32[]{:S(2)}) copy-start(f32[2,131072]{1,0:T(2,128)} %param.5) | copy-start | bytes 3145732
  0.6 11.5 %copy-start.4 = (f32[2,3,24]{2,0,1:T(2,128)S(1)}, f32[2,3,24]{2,0,1:T(2,128)}, u32[]{:S(2)}) copy-start(f32[2,3,24]{2,0,1:T(2,128)} %param.6) | copy-start | bytes 1732
  0.7 11.6 %copy-start.3 = (f32[2,4]{1,0:T(2,128)S(1)}, f32[2,4]{1,0:T(2,128)}, u32[]{:S(2)}) copy-start(f32[2,4]{1,0:T(2,128)} %rates.1) | copy-start | bytes 100
  0.7 11.6 %copy-start.2 = (s32[2,4]{1,0:T(2,128)S(1)}, s32[2,4]{1,0:T(2,128)}, u32[]{:S(2)}) copy-start(s32[2,4]{1,0:T(2,128)} %branches.1) | copy-start | bytes 100
  0.7 11.6 %copy-start.1 = (s32[2,4]{1,0:T(2,128)S(1)}, s32[2,4]{1,0:T(2,128)}, u32[]{:S(2)}) copy-start(s32[2,4]{1,0:T(2,128)} %targets.1) | copy-start | bytes 100
  0.7 30.5 %all-to-all-start = ((f32[128,16,128]{2,1,0:T(8,128)}), f32[128,16,128]{2,1,0:T(8,128)S(1)}, u32[]{:S(2)}, u32[]{:S(2)}) async-start(f32[128,16,128]{2,1,0:T(8,128)} %bitcast.18), calls=%async_computation | async-start | bytes 2097152 | tf_op jit(solution)/shard_map/all_to_all | solution.py:342
